TPU v7x, 256 devices: a whole 4x4x8 slice. The times are simulated.
256 devices in a mesh: rows: 8 (over y, core), cols: 16 (over z_hi, x), hub: 2 (over z_lo).
Axes of the slice: x: 4, y: 4, z: 8 (z_hi: 4, z_lo: 2; z = z_hi * 2 + z_lo), core: 2. Of those that a mesh axis runs over, the one named last changes fastest.
Arguments:
- light_bits: int32 [384, 12288], P('rows', 'cols'), may hold values from -2147483648 to 2147483647, as said below
- hub_bits: int32 [8, 12288], P('hub', 'cols'), may hold values from -2147483648 to 2147483647, as said below
- hub_ids: int32 [256], replicated, may hold values from 0 to 12287, as said below
Outputs:
- clustering: float32 [12288], P(('rows', 'cols'))
Inputs may be any that keep to these rules, and one draw needn't show every extreme that they name: Every word holds 32 bits; the matrix of light_bits is symmetric with a zero diagonal. `hub_bits`: every word holds 32 bits. `hub_ids`: 256 distinct vertex numbers.
All inputs are finite; a program needn't handle non-finite values.
Results may differ from a plain program's by a relative error of at most 0.0003.
Values sent between devices are 32-bit elements; how exact they have to be, the bound alone decides.
No kernel may reach another device: no remote copies, remote signals or barrier semaphores. Data moves between devices by JAX's collectives and lax.ppermute only.
A program may use at most 128 MiB of HBM per device.

v0:
```python
import jax
import jax.numpy as jnp
from jax import lax
from jax.experimental import pallas as pl
from jax.experimental.pallas import tpu as pltpu
from jax.sharding import Mesh
from jax.sharding import PartitionSpec as P

AXES = ("y", "core", "zh", "x", "zl")
ROWS = ("y", "core")
COLS = ("zh", "x")
SIZES = (4, 2, 4, 4, 2)
F8 = jnp.float8_e4m3fn
F32 = jnp.float32
I32 = jnp.int32
I8 = jnp.int8
BF16 = jnp.bfloat16
OUT = 96


def flat(y, core, zh, x, zl):
    return (((y * 2 + core) * 4 + zh) * 4 + x) * 2 + zl


def permutation(source_of):
    pairs = []
    for y in range(4):
        for core in range(2):
            for zh in range(4):
                for x in range(4):
                    for zl in range(2):
                        s = source_of(y, core, zh, x, zl)
                        if s is not None:
                            pairs.append((flat(*s), flat(y, core, zh, x, zl)))
    return pairs


FETCH = ((0, 1, 0, 1), (1, 0, 0, 1), (1, 0, 1, 0), (1, 0, 0, 1))
FETCH_BITS = sum(bit << (4 * r + g) for r, line in enumerate(FETCH) for g, bit in enumerate(line))


def group_of(y, z):
    return (-(y + z)) & 3


def fetch(y, core, zh, x, zl):
    z = 2 * zh + zl
    group = group_of(y, z)
    return (y, core, group, x, FETCH[(-y) & 3][group] ^ (z >> 2))


def partner(y, core, zh, x, zl):
    return (y, core, (zh + 1) % 4, x, 0) if zl == 1 else (y, core, (zh + 3) % 4, x, 1)


def along_y(y, core, zh, x, zl):
    return (group_of(y, 2 * zh + zl), core, zh, x, zl)


def unpack(words):
    n = words.shape[1]
    shifts = lax.broadcasted_iota(I32, (32, n), 0)
    rows = [
        jnp.right_shift(jnp.broadcast_to(words[i : i + 1, :], (32, n)), shifts)
        for i in range(words.shape[0])
    ]
    bits = jnp.concatenate(rows, 0).astype(I8) & I8(1)
    return bits.astype(BF16).astype(F8)


def place():
    y, core = lax.axis_index("y"), lax.axis_index("core")
    zh, x, zl = lax.axis_index("zh"), lax.axis_index("x"), lax.axis_index("zl")
    return y, core, zh, x, zl


def planes(words, bits):
    return jnp.concatenate([jnp.right_shift(words, b) & 1 for b in bits], 0)


def octets(words, at):
    return jnp.concatenate([jnp.right_shift(words, a) for a in at], 0).astype(I8)


def plane(bytes8, b):
    return (bytes8 & I8(SCALE[b])).astype(BF16).astype(F8)


SCALE = (1, 2, 4, 8, 16, 32, 64, -128)
OUTER = (((0,), (0,)), ((), ()))


def by_group(words, first):
    return jnp.where(first == 1, jnp.concatenate([words[4:8], words[0:4]], 0), words)


def right_kernel(words, rhs):
    for side in range(2):
        for part in range(6):
            rhs[256 * part : 256 * part + 256, 768 * side : 768 * side + 768] = unpack(
                words[48 * side + 8 * part : 48 * side + 8 * part + 8, :]
            )


def count_kernel(
    idp, pair, hubs, r0, rp, rm, r2, mine_rhs, other_rhs, out, keep, bits, lhs, near, turned, res
):
    y, core, zh, x, zl = place()
    row = 2 * y + core
    z = 2 * zh + zl
    group = (16 - y - z) & 3
    sources = ((r0, 0), (rp, 1), (rm, 3), (r2, 2))
    ids = idp[...]
    q = (lax.broadcasted_iota(I32, (256, 16), 1) == ids // 768).astype(BF16)
    r = (lax.broadcasted_iota(I32, (256, 768), 1) == ids % 768).astype(BF16)
    keep[...] = jnp.where(lax.dot_general(q, r, OUTER, preferred_element_type=F32) > 0.5, 0, -1)
    wordhot = (lax.broadcasted_iota(I32, (256, 48), 1) + 48 * row == ids // 32).astype(F32)
    bithot = (lax.broadcasted_iota(I32, (256, 32), 1) == ids % 32).astype(F32)
    light = 1.0 - lax.dot_general(
        wordhot.astype(BF16), bithot.astype(BF16), OUTER, preferred_element_type=F32
    )
    own = pl.ds(4 * zh + x, 1)
    side = pl.ds(4 * ((zh + 3 + 2 * zl) & 3) + x, 1)
    mine = jnp.concatenate([pair[0:48, :] & keep[own, :], pair[48:96, :] & keep[side, :]], 1)
    hub_words = jnp.concatenate(
        [
            by_group(hubs[0:8, :], zl) & keep[own, :],
            by_group(hubs[8:16, :], 1 - zl) & keep[side, :],
        ],
        1,
    )
    turn = jnp.right_shift(FETCH_BITS, 4 * ((4 - y) & 3) + group) & 1
    sent_by = turn ^ (z // 4)
    hub_col = planes(hub_words, range(32)).astype(F32)
    near[...] = hub_col.astype(F8)
    for p in range(4):
        xs = 2 * (core ^ (p // 2)) + p % 2
        rel = (4 + xs - x) & 3
        words = r0[...]
        for ref, k in sources[1:]:
            words = jnp.where(rel == k, ref[...], words)
        hub_rows = by_group(words[48:], sent_by)
        if p < 2:
            found = jnp.where(group == y, hub_rows, 0) & keep[pl.ds(2 * row + p, 1), :]
            turned[768 * p : 768 * p + 768, :] = jnp.concatenate([found] * 16, 0).T
        line = keep[pl.ds(4 * group + xs, 1), :]
        bits[56 * p : 56 * p + 48, :] = words[:48] & line
        bits[56 * p + 48 : 56 * p + 56, :] = hub_rows & line
    lane = lax.broadcasted_iota(I32, (48, 128), 1) // 8
    first = (zl == 0).astype(F32)
    once = ((x == 0) & (z == ((16 - 2 * y) & 3))).astype(F32)

    def fill(tile):
        for p in range(4):
            at = slice(768 * p, 768 * p + 768)
            if tile < 0:
                words = octets(bits[56 * p + 48 : 56 * p + 56, :], (0, 8, 16, 24))
                for b in range(8):
                    lhs[1, 32 * b : 32 * b + 32, at] = plane(words, b)
            else:
                half, quarter = tile // 2, tile % 2
                words = octets(bits[56 * p : 56 * p + 48, :], (16 * half, 16 * half + 8))
                for b in range(4):
                    lhs[tile % 2, 96 * b : 96 * b + 96, at] = plane(words, 4 * quarter + b)

    def product(tile, size):
        return jnp.dot(
            lhs[tile % 2, :size, :1536], mine_rhs[...], preferred_element_type=F32
        ) + jnp.dot(lhs[tile % 2, :size, 1536:], other_rhs[...], preferred_element_type=F32)

    fill(-1)
    hub_paths = product(-1, 256)
    fill(0)
    hub_tri = jnp.concatenate(
        [
            jnp.sum(
                hub_paths[32 * b + 8 * s : 32 * b + 8 * s + 8, :]
                * hub_col[64 * s + 8 * b : 64 * s + 8 * b + 8, :],
                axis=1,
                keepdims=True,
            )
            for s in range(4)
            for b in range(8)
        ],
        0,
    )
    bit = (lax.broadcasted_iota(I32, (256, 1), 0) // 8) & 7
    unscale = jnp.right_shift(128, bit).astype(F32) * jnp.where(bit == 7, -0.5 / 128, 0.5 / 128)
    hub_tri = unscale * hub_tri
    hub_deg = first * jnp.sum(hub_col[:, :768], axis=1, keepdims=True)
    hub_part = lax.dot_general(
        wordhot,
        jnp.concatenate([hub_tri * bithot, hub_deg * bithot], 1),
        OUTER,
        precision=lax.Precision.HIGHEST,
        preferred_element_type=F32,
    )
    for tile in range(4):
        half, quarter = tile // 2, tile % 2
        paths = product(tile, 384)
        if tile < 3:
            fill(tile + 1)
        both = octets(mine, (16 * half, 16 * half + 8))
        edges = jnp.concatenate([plane(both, 4 * quarter + b) for b in range(4)], 0)
        reach = lax.dot_general(
            edges, near[...], (((1,), (1,)), ((), ())), preferred_element_type=F32
        )
        for b in range(4):
            scale = 1.0 / SCALE[4 * quarter + b]
            for k in range(2):
                at = 16 * half + 8 * k + 4 * quarter + b
                rows = slice(96 * b + 48 * k, 96 * b + 48 * k + 48)
                words = turned[pl.ds(at, 48, stride=32), :]
                low = (jnp.right_shift(words, lane) & 1).astype(F32)
                high = (jnp.right_shift(words, lane + 16) & 1).astype(F32)
                edge = (jnp.right_shift(mine, at) & 1).astype(F32)
                closed = jnp.sum(paths[rows, :] * edge, axis=1, keepdims=True)
                with_hub = jnp.sum(
                    reach[rows, :128] * low + reach[rows, 128:] * high, axis=1, keepdims=True
                )
                res[:, at : at + 1] = (0.5 * scale) * closed + scale * with_hub
                res[:, 32 + at : 33 + at] = first * jnp.sum(
                    edge[:, :768], axis=1, keepdims=True
                ) + once * jnp.sum(low + high, axis=1, keepdims=True)
    total = res[...] * jnp.concatenate([light, light], 1) + hub_part
    for c in range(16):
        line = jnp.concatenate(
            [total[3 * c + k : 3 * c + k + 1, 0:32] for k in range(3)]
            + [jnp.zeros((1, 32), F32)]
            + [total[3 * c + k : 3 * c + k + 1, 32:64] for k in range(3)]
            + [jnp.zeros((1, 32), F32)],
            1,
        )
        out[2 * c : 2 * c + 1, :] = line
        out[2 * c + 1 : 2 * c + 2, :] = line


def call(kernel, outs, scratch, args, flops, limit):
    vmem = pl.BlockSpec(memory_space=pltpu.VMEM)
    return pl.pallas_call(
        kernel,
        out_shape=[jax.ShapeDtypeStruct(*o) for o in outs],
        in_specs=[vmem] * len(args),
        out_specs=[vmem] * len(outs),
        scratch_shapes=scratch,
        cost_estimate=pl.CostEstimate(flops=flops, bytes_accessed=1 << 20, transcendentals=0),
        compiler_params=pltpu.CompilerParams(vmem_limit_bytes=limit * 2**20),
    )(*args)


def clustering(light_bits, hub_bits, hub_ids):
    def send(value, source):
        return lax.ppermute(value, AXES, perm=permutation(source))

    rows = send(light_bits, fetch)
    beside = send(light_bits, partner)
    twin = send(hub_bits, lambda y, core, zh, x, zl: (y, core, zh, x, zl ^ 1))
    hub = jnp.concatenate([hub_bits, twin], 0)
    hub_rows = send(hub, fetch)
    hub_beside = send(hub, partner)
    rows = jnp.concatenate([rows, hub_rows], 0)
    ring = [
        send(rows, lambda y, core, zh, x, zl, r=r: (y, core, zh, (x + r) % 4, zl))
        for r in (1, 3, 2)
    ]
    pair = jnp.concatenate([light_bits, beside], 0)
    hubs = jnp.concatenate([hub, hub_beside], 0)
    yy = send(pair, along_y)
    yc = send(yy, lambda y, core, zh, x, zl: (y, core ^ 1, zh, x, zl))
    planed = hub_ids.reshape(8, 32).T.reshape(256, 1)
    sides = []
    for words in (yy, yc):
        sides += call(right_kernel, [((1536, 1536), F8)], [], (words,), 1 << 29, 8)
    (table,) = call(
        count_kernel,
        [((32, 256), F32)],
        [
            pltpu.VMEM((16, 768), I32),
            pltpu.VMEM((224, 768), I32),
            pltpu.VMEM((2, 384, 3072), F8),
            pltpu.VMEM((256, 1536), F8),
            pltpu.VMEM((1536, 128), I32),
            pltpu.VMEM((48, 64), F32),
        ],
        (planed, pair, hubs, rows, *ring, *sides),
        1 << 33,
        24,
    )
    everyone = lax.all_to_all(table, ("zh", "x", "zl"), 0, 0, tiled=True)
    total = jnp.sum(everyone, axis=0)
    return total[:OUT] / (1.0 + total[128 : 128 + OUT])


def solution(mesh):
    finer = Mesh(mesh.devices.reshape(SIZES), AXES)
    placed = (P(ROWS, COLS), P("zl", COLS), P())
    return jax.shard_map(
        clustering, mesh=finer, in_specs=placed, out_specs=P(ROWS + COLS), check_vma=False
    )
```

profile of v0, /device:TPU:8, one launch (start us, length us, event | category | flops | bytes accessed | tf_op | source)
XLA Modules:
  0.0 70.0 jit_solution(15134415170821556130)
XLA Ops:
  0.0 5.9 %collective-permute-start = (s32[48,768]{1,0:T(8,128)}, s32[48,768]{1,0:T(8,128)S(1)}, u32[]{:S(2)}, u32[]{:S(2)}) collective-permute-start(s32[48,768]{1,0:T(8,128)} %param.3), channel_id=1, source_target_pairs={{25,0},{8,1},{27,2},{10,3},{29,4},{12,5},{31,6},{14,7},{1,8},{16,9... | collective-permute-start | bytes 442376 | tf_op jit(solution)/shard_map/ppermute | solution.py:253
  5.9 1.0 %constant_dynamic-update-slice_fusion.1 = s32[96,768]{1,0:T(8,128)S(1)} fusion(s32[48,768]{1,0:T(8,128)} %param.3), kind=kLoop, calls=%fused_computation.3 | loop fusion | bytes 294912
  6.8 3.1 %collective-permute-done = s32[48,768]{1,0:T(8,128)S(1)} collective-permute-done((s32[48,768]{1,0:T(8,128)}, s32[48,768]{1,0:T(8,128)S(1)}, u32[]{:S(2)}, u32[]{:S(2)}) %collective-permute-start) | collective-permute-done | bytes 147488 | tf_op jit(solution)/shard_map/ppermute | solution.py:253
  9.9 4.2 %collective-permute-start.8 = (s32[96,768]{1,0:T(8,128)S(1)}, s32[96,768]{1,0:T(8,128)S(1)}, u32[]{:S(2)}, u32[]{:S(2)}) collective-permute-start(s32[96,768]{1,0:T(8,128)S(1)} %constant_dynamic-update-slice_fusion.pair), channel_id=1, source_target_pairs={{0,0},{193,1},{2,2},{195,3},{4,4},{197,5},{6,6},{199,7},{136,8},{7... | collective-permute-start | bytes 884744 | tf_op jit(solution)/shard_map/ppermute | solution.py:253
  14.1 3.0 %collective-permute-start.3 = (s32[48,768]{1,0:T(8,128)}, s32[48,768]{1,0:T(8,128)S(1)}, u32[]{:S(2)}, u32[]{:S(2)}) collective-permute-start(s32[48,768]{1,0:T(8,128)} %param.3), channel_id=1, source_target_pairs={{0,0},{25,1},{2,2},{27,3},{4,4},{29,5},{6,6},{31,7},{16,8},{9,9},{... | collective-permute-start | bytes 442376 | tf_op jit(solution)/shard_map/ppermute | solution.py:253
  17.2 0.1 collective-permute-start.1
  17.3 0.8 %reshape.8 = s32[8,32]{1,0:T(8,128)S(1)} reshape(s32[256]{0:T(256)} %param.5) | data formatting | bytes 2048 | tf_op jit(solution)/shard_map/reshape | solution.py:270
  18.0 0.1 copy.6
  18.1 0.1 reshape.10.idp
  18.2 3.0 %collective-permute-done.1 = s32[4,768]{1,0:T(4,128)S(1)} collective-permute-done((s32[4,768]{1,0:T(4,128)}, s32[4,768]{1,0:T(4,128)S(1)}, u32[]{:S(2)}, u32[]{:S(2)}) %collective-permute-start.1) | collective-permute-done | bytes 12320 | tf_op jit(solution)/shard_map/ppermute | solution.py:253
  21.2 0.7 %pad_add_fusion.1 = s32[8,768]{1,0:T(8,128)S(1)} fusion(s32[4,768]{1,0:T(4,128)S(1)} %collective-permute-done.1, s32[4,768]{1,0:T(4,128)} %param.4), kind=kLoop, calls=%fused_computation.1 | loop fusion | flops 6144 | bytes 49152 | tf_op jit(solution)/shard_map/concatenate | solution.py:258
  21.9 4.2 %collective-permute-start.4 = (s32[8,768]{1,0:T(8,128)S(1)}, s32[8,768]{1,0:T(8,128)S(1)}, u32[]{:S(2)}, u32[]{:S(2)}) collective-permute-start(s32[8,768]{1,0:T(8,128)S(1)} %pad_add_fusion.1), channel_id=1, source_target_pairs={{0,0},{25,1},{2,2},{27,3},{4,4},{29,5},{6,6},{31,7},{16,8},{9,9},{... | collective-permute-start | bytes 73736 | tf_op jit(solution)/shard_map/ppermute | solution.py:253
  26.1 1.0 %collective-permute-start.2 = (s32[8,768]{1,0:T(8,128)S(1)}, s32[8,768]{1,0:T(8,128)S(1)}, u32[]{:S(2)}, u32[]{:S(2)}) collective-permute-start(s32[8,768]{1,0:T(8,128)S(1)} %pad_add_fusion.1), channel_id=1, source_target_pairs={{25,0},{8,1},{27,2},{10,3},{29,4},{12,5},{31,6},{14,7},{1,8},{16,9... | collective-permute-start | bytes 73736 | tf_op jit(solution)/shard_map/ppermute | solution.py:253
  27.1 0.0 collective-permute-done.8.words
  27.1 0.0 collective-permute-start.9
  27.1 0.0 collective-permute-done.3
  27.1 1.7 %collective-permute-done.4 = s32[8,768]{1,0:T(8,128)S(1)} collective-permute-done((s32[8,768]{1,0:T(8,128)S(1)}, s32[8,768]{1,0:T(8,128)S(1)}, u32[]{:S(2)}, u32[]{:S(2)}) %collective-permute-start.4) | collective-permute-done | bytes 24608 | tf_op jit(solution)/shard_map/ppermute | solution.py:253
  28.8 2.8 %collective-permute-start.5 = (s32[56,768]{1,0:T(8,128)S(1)}, s32[56,768]{1,0:T(8,128)S(1)}, u32[]{:S(2)}, u32[]{:S(2)}) collective-permute-start(s32[56,768]{1,0:T(8,128)S(1)} %constant_dynamic-update-slice_fusion.2.r0), channel_id=1, source_target_pairs={{2,0},{3,1},{4,2},{5,3},{6,4},{7,5},{0,6},{1,7},{10,8},{11,9},{12,... | collective-permute-start | bytes 516104 | tf_op jit(solution)/shard_map/ppermute | solution.py:253
  31.6 0.0 collective-permute-start.6
  31.6 2.3 %collective-permute-start.7 = (s32[56,768]{1,0:T(8,128)S(1)}, s32[56,768]{1,0:T(8,128)S(1)}, u32[]{:S(2)}, u32[]{:S(2)}) collective-permute-start(s32[56,768]{1,0:T(8,128)S(1)} %constant_dynamic-update-slice_fusion.2.r0), channel_id=1, source_target_pairs={{4,0},{5,1},{6,2},{7,3},{0,4},{1,5},{2,6},{3,7},{12,8},{13,9},{14,... | collective-permute-start | bytes 516104 | tf_op jit(solution)/shard_map/ppermute | solution.py:253
  33.9 0.0 collective-permute-done.2
  33.9 0.7 %pad_add_fusion.hubs = s32[16,768]{1,0:T(8,128)S(1)} fusion(s32[8,768]{1,0:T(8,128)S(1)} %collective-permute-done.2, s32[4,768]{1,0:T(4,128)S(1)} %collective-permute-done.1, s32[4,768]{1,0:T(4,128)} %param.4), kind=kLoop, calls=%fused_computation | loop fusion | flops 24576 | bytes 98304 | tf_op jit(solution)/shard_map/concatenate | solution.py:267
  34.6 0.7 shard_map.37.mine_rhs
  35.3 0.0 collective-permute-done.9.words
  35.3 0.7 shard_map.38.other_rhs
  36.0 0.4 collective-permute-done.5.rp
  36.4 5.0 %collective-permute-done.6.rm = s32[56,768]{1,0:T(8,128)S(1)} collective-permute-done((s32[56,768]{1,0:T(8,128)S(1)}, s32[56,768]{1,0:T(8,128)S(1)}, u32[]{:S(2)}, u32[]{:S(2)}) %collective-permute-start.6) | collective-permute-done | bytes 172064 | tf_op jit(solution)/shard_map/ppermute | solution.py:253
  41.4 0.0 collective-permute-done.7.r2
  41.4 11.0 %shard_map.39 = f32[32,256]{1,0:T(8,128)S(1)} custom-call(s32[256,1]{1,0:T(8,128)S(1)} %reshape.10.idp, s32[96,768]{1,0:T(8,128)S(1)} %constant_dynamic-update-slice_fusion.pair, s32[16,768]{1,0:T(8,128)S(1)} %pad_add_fusion.hubs, s32[56,768]{1,0:T(8,128)S(1)} %constant_dynamic-update-slice_fusion.2.r0, s32[56,768]{1,0:T(8,128)S(1)} %collective-permute-done.5.rp, ...), custom_call_target="tpu_custom_call" | custom-call | flops 8589934592 | bytes 1048576 | tf_op jit(solution)/shard_map/pallas_call | solution.py:240
  52.5 16.9 %all_to_all.9 = f32[32,1,256]{2,1,0:T(1,128)S(1)} all-to-all(f32[32,1,256]{2,1,0:T(1,128)S(1)} %copy.8), channel_id=1, replica_groups=mesh['y'=4,'core'=2,'zh'=4,'x'=4,'zl'=2] {'zh','x','zl'}, dimensions={0} | all-to-all | bytes 65536 | tf_op jit(solution)/shard_map/all_to_all | solution.py:289
  69.4 0.1 reduce_sum.9
  69.5 0.5 add_divide_fusion
  (4 shorter events, 0.1 us)
Async XLA Ops:
  0.0 9.9 %collective-permute-start = (s32[48,768]{1,0:T(8,128)}, s32[48,768]{1,0:T(8,128)S(1)}, u32[]{:S(2)}, u32[]{:S(2)}) collective-permute-start(s32[48,768]{1,0:T(8,128)} %param.3), channel_id=1, source_target_pairs={{25,0},{8,1},{27,2},{10,3},{29,4},{12,5},{31,6},{14,7},{1,8},{16,9... | collective-permute-start | bytes 442376 | tf_op jit(solution)/shard_map/ppermute | solution.py:253
  9.9 17.2 %collective-permute-start.8 = (s32[96,768]{1,0:T(8,128)S(1)}, s32[96,768]{1,0:T(8,128)S(1)}, u32[]{:S(2)}, u32[]{:S(2)}) collective-permute-start(s32[96,768]{1,0:T(8,128)S(1)} %constant_dynamic-update-slice_fusion.pair), channel_id=1, source_target_pairs={{0,0},{193,1},{2,2},{195,3},{4,4},{197,5},{6,6},{199,7},{136,8},{7... | collective-permute-start | bytes 884744 | tf_op jit(solution)/shard_map/ppermute | solution.py:253
  14.1 13.0 %collective-permute-start.3 = (s32[48,768]{1,0:T(8,128)}, s32[48,768]{1,0:T(8,128)S(1)}, u32[]{:S(2)}, u32[]{:S(2)}) collective-permute-start(s32[48,768]{1,0:T(8,128)} %param.3), channel_id=1, source_target_pairs={{0,0},{25,1},{2,2},{27,3},{4,4},{29,5},{6,6},{31,7},{16,8},{9,9},{... | collective-permute-start | bytes 442376 | tf_op jit(solution)/shard_map/ppermute | solution.py:253
  17.2 4.0 %collective-permute-start.1 = (s32[4,768]{1,0:T(4,128)}, s32[4,768]{1,0:T(4,128)S(1)}, u32[]{:S(2)}, u32[]{:S(2)}) collective-permute-start(s32[4,768]{1,0:T(4,128)} %param.4), channel_id=1, source_target_pairs={{1,0},{0,1},{3,2},{2,3},{5,4},{4,5},{7,6},{6,7},{9,8},{8,9},{11,10... | collective-permute-start | bytes 36872 | tf_op jit(solution)/shard_map/ppermute | solution.py:253
  21.9 6.9 %collective-permute-start.4 = (s32[8,768]{1,0:T(8,128)S(1)}, s32[8,768]{1,0:T(8,128)S(1)}, u32[]{:S(2)}, u32[]{:S(2)}) collective-permute-start(s32[8,768]{1,0:T(8,128)S(1)} %pad_add_fusion.1), channel_id=1, source_target_pairs={{0,0},{25,1},{2,2},{27,3},{4,4},{29,5},{6,6},{31,7},{16,8},{9,9},{... | collective-permute-start | bytes 73736 | tf_op jit(solution)/shard_map/ppermute | solution.py:253
  26.1 7.8 %collective-permute-start.2 = (s32[8,768]{1,0:T(8,128)S(1)}, s32[8,768]{1,0:T(8,128)S(1)}, u32[]{:S(2)}, u32[]{:S(2)}) collective-permute-start(s32[8,768]{1,0:T(8,128)S(1)} %pad_add_fusion.1), channel_id=1, source_target_pairs={{25,0},{8,1},{27,2},{10,3},{29,4},{12,5},{31,6},{14,7},{1,8},{16,9... | collective-permute-start | bytes 73736 | tf_op jit(solution)/shard_map/ppermute | solution.py:253
  27.1 8.2 %collective-permute-start.9 = (s32[96,768]{1,0:T(8,128)S(1)}, s32[96,768]{1,0:T(8,128)S(1)}, u32[]{:S(2)}, u32[]{:S(2)}) collective-permute-start(s32[96,768]{1,0:T(8,128)S(1)} %collective-permute-done.8.words), channel_id=1, source_target_pairs={{32,0},{33,1},{34,2},{35,3},{36,4},{37,5},{38,6},{39,7},{40,8},{41... | collective-permute-start | bytes 884744 | tf_op jit(solution)/shard_map/ppermute | solution.py:253
  28.8 7.6 %collective-permute-start.5 = (s32[56,768]{1,0:T(8,128)S(1)}, s32[56,768]{1,0:T(8,128)S(1)}, u32[]{:S(2)}, u32[]{:S(2)}) collective-permute-start(s32[56,768]{1,0:T(8,128)S(1)} %constant_dynamic-update-slice_fusion.2.r0), channel_id=1, source_target_pairs={{2,0},{3,1},{4,2},{5,3},{6,4},{7,5},{0,6},{1,7},{10,8},{11,9},{12,... | collective-permute-start | bytes 516104 | tf_op jit(solution)/shard_map/ppermute | solution.py:253
  31.6 9.8 %collective-permute-start.6 = (s32[56,768]{1,0:T(8,128)S(1)}, s32[56,768]{1,0:T(8,128)S(1)}, u32[]{:S(2)}, u32[]{:S(2)}) collective-permute-start(s32[56,768]{1,0:T(8,128)S(1)} %constant_dynamic-update-slice_fusion.2.r0), channel_id=1, source_target_pairs={{6,0},{7,1},{0,2},{1,3},{2,4},{3,5},{4,6},{5,7},{14,8},{15,9},{8,1... | collective-permute-start | bytes 516104 | tf_op jit(solution)/shard_map/ppermute | solution.py:253
  31.6 9.8 %collective-permute-start.7 = (s32[56,768]{1,0:T(8,128)S(1)}, s32[56,768]{1,0:T(8,128)S(1)}, u32[]{:S(2)}, u32[]{:S(2)}) collective-permute-start(s32[56,768]{1,0:T(8,128)S(1)} %constant_dynamic-update-slice_fusion.2.r0), channel_id=1, source_target_pairs={{4,0},{5,1},{6,2},{7,3},{0,4},{1,5},{2,6},{3,7},{12,8},{13,9},{14,... | collective-permute-start | bytes 516104 | tf_op jit(solution)/shard_map/ppermute | solution.py:253
where the time goes:
time: 70.4 us; the launch traced here: 70 us
  starting transfers between devices  23.5 us (33%)
  blocking collectives  16.9 us (24%)
  waiting for transfers between devices  13.1 us (19%)
  Pallas kernels  12.4 us (18%)
  other arithmetic  2.01 us (3%)
  local copies, waits for them, and re-layouts  1.94 us (3%)
    ppermute x10, starting transfers between devices, send(): return lax.ppermute(value, AXES, perm=permutation(source))  23.5 us
    all_to_all x1, blocking collectives, clustering(): everyone = lax.all_to_all(table, ('zh', 'x', 'zl'), 0, 0, tiled=True)  16.9 us
    ppermute x10, waiting for transfers between devices, send(): return lax.ppermute(value, AXES, perm=permutation(source))  13.1 us
    pallas_call x3, Pallas kernels, call(): pl.pallas_call(kernel, out_shape=[jax.ShapeDtypeStruct(*o) for o in outs]...  12.4 us
  transfers between devices with their start and end apart: 10, of which 5 were waited for; matrix products, arithmetic and copies ran while one was open for 5% of the time, Pallas kernels for 2%

commit v1 on v0

--- a/solution.py
+++ b/solution.py
@@ -36,7 +36,6 @@
 
 
 FETCH = ((0, 1, 0, 1), (1, 0, 0, 1), (1, 0, 1, 0), (1, 0, 0, 1))
-FETCH_BITS = sum(bit << (4 * r + g) for r, line in enumerate(FETCH) for g, bit in enumerate(line))
 
 
 def group_of(y, z):
@@ -88,10 +87,6 @@
 
 SCALE = (1, 2, 4, 8, 16, 32, 64, -128)
 OUTER = (((0,), (0,)), ((), ()))
-
-
-def by_group(words, first):
-    return jnp.where(first == 1, jnp.concatenate([words[4:8], words[0:4]], 0), words)
 
 
 def right_kernel(words, rhs):
@@ -123,14 +118,8 @@
     side = pl.ds(4 * ((zh + 3 + 2 * zl) & 3) + x, 1)
     mine = jnp.concatenate([pair[0:48, :] & keep[own, :], pair[48:96, :] & keep[side, :]], 1)
     hub_words = jnp.concatenate(
-        [
-            by_group(hubs[0:8, :], zl) & keep[own, :],
-            by_group(hubs[8:16, :], 1 - zl) & keep[side, :],
-        ],
-        1,
-    )
-    turn = jnp.right_shift(FETCH_BITS, 4 * ((4 - y) & 3) + group) & 1
-    sent_by = turn ^ (z // 4)
+        [hubs[0:8, :] & keep[own, :], hubs[8:16, :] & keep[side, :]], 1
+    )
     hub_col = planes(hub_words, range(32)).astype(F32)
     near[...] = hub_col.astype(F8)
     for p in range(4):
@@ -139,13 +128,10 @@
         words = r0[...]
         for ref, k in sources[1:]:
             words = jnp.where(rel == k, ref[...], words)
-        hub_rows = by_group(words[48:], sent_by)
         if p < 2:
-            found = jnp.where(group == y, hub_rows, 0) & keep[pl.ds(2 * row + p, 1), :]
+            found = jnp.where(group == y, words[48:], 0) & keep[pl.ds(2 * row + p, 1), :]
             turned[768 * p : 768 * p + 768, :] = jnp.concatenate([found] * 16, 0).T
-        line = keep[pl.ds(4 * group + xs, 1), :]
-        bits[56 * p : 56 * p + 48, :] = words[:48] & line
-        bits[56 * p + 48 : 56 * p + 56, :] = hub_rows & line
+        bits[56 * p : 56 * p + 56, :] = words & keep[pl.ds(4 * group + xs, 1), :]
     lane = lax.broadcasted_iota(I32, (48, 128), 1) // 8
     first = (zl == 0).astype(F32)
     once = ((x == 0) & (z == ((16 - 2 * y) & 3))).astype(F32)
@@ -249,13 +235,16 @@
 
 
 def clustering(light_bits, hub_bits, hub_ids):
+    _, _, _, _, zl = place()
+
     def send(value, source):
         return lax.ppermute(value, AXES, perm=permutation(source))
 
     rows = send(light_bits, fetch)
     beside = send(light_bits, partner)
     twin = send(hub_bits, lambda y, core, zh, x, zl: (y, core, zh, x, zl ^ 1))
-    hub = jnp.concatenate([hub_bits, twin], 0)
+    even = zl == 0
+    hub = jnp.concatenate([jnp.where(even, hub_bits, twin), jnp.where(even, twin, hub_bits)], 0)
     hub_rows = send(hub, fetch)
     hub_beside = send(hub, partner)
     rows = jnp.concatenate([rows, hub_rows], 0)

time: 70.4 us -> 64.1 us (0.911)
  waiting for transfers between devices: 13.1 us -> 9.46 us
  blocking collectives: 16.9 us -> 14.3 us
    ppermute x10, waiting for transfers between devices: 13.1 us -> 9.46 us  [send(): return lax.ppermute(value, AXES, perm=permutation(source))]
    all_to_all x1, blocking collectives: 16.9 us -> 14.3 us  [clustering(): everyone = lax.all_to_all(table, ('zh', 'x', 'zl'), 0, 0, tiled=True)]
    ppermute x10, starting transfers between devices: 23.5 us -> 24.2 us  [send(): return lax.ppermute(value, AXES, perm=permutation(source))]
    select_n x0 -> x1, other arithmetic: none -> 0.72 us  [clustering(): jnp.where(even, hub_bits, twin)]
    concatenate x1, other arithmetic: 0.72 us -> 0.01 us  [clustering(): hubs = jnp.concatenate([hub, hub_beside], 0)]
    concatenate x1, other arithmetic: 0.72 us -> 0.01 us  [clustering(): jnp.concatenate([jnp.where(even, hub_bits, twin), jnp.where(even, twin, h...]
  transfers between devices with their start and end apart: 10 -> 10, of which waited for: 5 -> 4; matrix products, arithmetic and copies ran while one was open for 5% -> 4% of each run, Pallas kernels for 2% -> 2%
where the time goes in v1:
time: 64.1 us; the launch traced here: 63.8 us
  starting transfers between devices  24.2 us (38%)
  blocking collectives  14.3 us (22%)
  Pallas kernels  12.4 us (19%)
  waiting for transfers between devices  9.46 us (15%)
  local copies, waits for them, and re-layouts  1.91 us (3%)
  other arithmetic  1.32 us (2%)
    ppermute x10, starting transfers between devices, send(): return lax.ppermute(value, AXES, perm=permutation(source))  24.2 us
    all_to_all x1, blocking collectives, clustering(): everyone = lax.all_to_all(table, ('zh', 'x', 'zl'), 0, 0, tiled=True)  14.3 us
    pallas_call x3, Pallas kernels, call(): pl.pallas_call(kernel, out_shape=[jax.ShapeDtypeStruct(*o) for o in outs]...  12.4 us
    ppermute x10, waiting for transfers between devices, send(): return lax.ppermute(value, AXES, perm=permutation(source))  9.46 us
  transfers between devices with their start and end apart: 10, of which 4 were waited for; matrix products, arithmetic and copies ran while one was open for 4% of the time, Pallas kernels for 2%

profile of v1, /device:TPU:8, one launch (start us, length us, event | category | flops | bytes accessed | tf_op | source)
XLA Modules:
  0.0 63.8 jit_solution(16141393906173426811)
XLA Ops:
  0.0 5.9 %collective-permute-start = (s32[48,768]{1,0:T(8,128)}, s32[48,768]{1,0:T(8,128)S(1)}, u32[]{:S(2)}, u32[]{:S(2)}) collective-permute-start(s32[48,768]{1,0:T(8,128)} %param.3), channel_id=1, source_target_pairs={{25,0},{8,1},{27,2},{10,3},{29,4},{12,5},{31,6},{14,7},{1,8},{16,9... | collective-permute-start | bytes 442376 | tf_op jit(solution)/shard_map/ppermute | solution.py:241
  5.9 1.9 %collective-permute-start.3 = (s32[48,768]{1,0:T(8,128)}, s32[48,768]{1,0:T(8,128)S(1)}, u32[]{:S(2)}, u32[]{:S(2)}) collective-permute-start(s32[48,768]{1,0:T(8,128)} %param.3), channel_id=1, source_target_pairs={{0,0},{25,1},{2,2},{27,3},{4,4},{29,5},{6,6},{31,7},{16,8},{9,9},{... | collective-permute-start | bytes 442376 | tf_op jit(solution)/shard_map/ppermute | solution.py:241
  7.8 2.5 %collective-permute-start.1 = (s32[4,768]{1,0:T(4,128)}, s32[4,768]{1,0:T(4,128)S(1)}, u32[]{:S(2)}, u32[]{:S(2)}) collective-permute-start(s32[4,768]{1,0:T(4,128)} %param.4), channel_id=1, source_target_pairs={{1,0},{0,1},{3,2},{2,3},{5,4},{4,5},{7,6},{6,7},{9,8},{8,9},{11,10... | collective-permute-start | bytes 36872 | tf_op jit(solution)/shard_map/ppermute | solution.py:241
  10.3 0.8 %reshape.8 = s32[8,32]{1,0:T(8,128)S(1)} reshape(s32[256]{0:T(256)} %param.5) | data formatting | bytes 2048 | tf_op jit(solution)/shard_map/reshape | solution.py:259
  11.1 0.1 copy.6
  11.1 0.1 reshape.10.idp
  11.3 0.9 %constant_dynamic-update-slice_fusion.1 = s32[96,768]{1,0:T(8,128)S(1)} fusion(s32[48,768]{1,0:T(8,128)} %param.3), kind=kLoop, calls=%fused_computation.3 | loop fusion | bytes 294912
  12.2 0.0 collective-permute-done
  12.2 3.7 %collective-permute-start.8 = (s32[96,768]{1,0:T(8,128)S(1)}, s32[96,768]{1,0:T(8,128)S(1)}, u32[]{:S(2)}, u32[]{:S(2)}) collective-permute-start(s32[96,768]{1,0:T(8,128)S(1)} %constant_dynamic-update-slice_fusion.pair), channel_id=1, source_target_pairs={{0,0},{193,1},{2,2},{195,3},{4,4},{197,5},{6,6},{199,7},{136,8},{7... | collective-permute-start | bytes 884744 | tf_op jit(solution)/shard_map/ppermute | solution.py:241
  15.9 0.0 collective-permute-done.1
  15.9 0.7 %broadcast_select_fusion.1 = (s32[4,768]{1,0:T(4,128)S(1)}, s32[4,768]{1,0:T(4,128)S(1)}) fusion(s32[4,768]{1,0:T(4,128)} %param.4, s32[4,768]{1,0:T(4,128)S(1)} %collective-permute-done.1, pred[]{:T(512)S(6)} %eq.3), kind=kLoop, calls=%fused_computation.7 | loop fusion | flops 6144 | bytes 49153 | tf_op jit(solution)/shard_map/jit(_where)/select_n | solution.py:247
  16.6 0.1 collective-permute-start.2
  16.8 5.1 %collective-permute-start.4 = (s32[8,768]{1,0:T(8,128)S(1)}, s32[8,768]{1,0:T(8,128)S(1)}, u32[]{:S(2)}, u32[]{:S(2)}) collective-permute-start(s32[8,768]{1,0:T(8,128)S(1)} %pad_add_fusion.1), channel_id=1, source_target_pairs={{0,0},{25,1},{2,2},{27,3},{4,4},{29,5},{6,6},{31,7},{16,8},{9,9},{... | collective-permute-start | bytes 73736 | tf_op jit(solution)/shard_map/ppermute | solution.py:241
  21.9 1.7 %collective-permute-done.8.words = s32[96,768]{1,0:T(8,128)S(1)} collective-permute-done((s32[96,768]{1,0:T(8,128)S(1)}, s32[96,768]{1,0:T(8,128)S(1)}, u32[]{:S(2)}, u32[]{:S(2)}) %collective-permute-start.8) | collective-permute-done | bytes 294944 | tf_op jit(solution)/shard_map/ppermute | solution.py:241
  23.5 0.0 collective-permute-start.9
  23.5 0.0 collective-permute-done.3
  23.5 0.1 collective-permute-done.4
  23.7 2.8 %collective-permute-start.5 = (s32[56,768]{1,0:T(8,128)S(1)}, s32[56,768]{1,0:T(8,128)S(1)}, u32[]{:S(2)}, u32[]{:S(2)}) collective-permute-start(s32[56,768]{1,0:T(8,128)S(1)} %constant_dynamic-update-slice_fusion.2.r0), channel_id=1, source_target_pairs={{2,0},{3,1},{4,2},{5,3},{6,4},{7,5},{0,6},{1,7},{10,8},{11,9},{12,... | collective-permute-start | bytes 516104 | tf_op jit(solution)/shard_map/ppermute | solution.py:241
  26.4 0.0 collective-permute-start.6
  26.5 2.3 %collective-permute-start.7 = (s32[56,768]{1,0:T(8,128)S(1)}, s32[56,768]{1,0:T(8,128)S(1)}, u32[]{:S(2)}, u32[]{:S(2)}) collective-permute-start(s32[56,768]{1,0:T(8,128)S(1)} %constant_dynamic-update-slice_fusion.2.r0), channel_id=1, source_target_pairs={{4,0},{5,1},{6,2},{7,3},{0,4},{1,5},{2,6},{3,7},{12,8},{13,9},{14,... | collective-permute-start | bytes 516104 | tf_op jit(solution)/shard_map/ppermute | solution.py:241
  28.7 0.0 collective-permute-done.2
  28.8 0.7 %shard_map.37.mine_rhs = f8e4m3fn[1536,1536]{1,0:T(32,128)(4,1)S(1)} custom-call(s32[96,768]{1,0:T(8,128)S(1)} %collective-permute-done.8.words), custom_call_target="tpu_custom_call" | custom-call | flops 536870912 | bytes 1048576 | tf_op jit(solution)/shard_map/pallas_call | solution.py:226
  29.5 0.0 collective-permute-done.9.words
  29.5 0.7 %shard_map.38.other_rhs = f8e4m3fn[1536,1536]{1,0:T(32,128)(4,1)S(1)} custom-call(s32[96,768]{1,0:T(8,128)S(1)} %collective-permute-done.9.words), custom_call_target="tpu_custom_call" | custom-call | flops 536870912 | bytes 1048576 | tf_op jit(solution)/shard_map/pallas_call | solution.py:226
  30.2 4.3 %collective-permute-done.5.rp = s32[56,768]{1,0:T(8,128)S(1)} collective-permute-done((s32[56,768]{1,0:T(8,128)S(1)}, s32[56,768]{1,0:T(8,128)S(1)}, u32[]{:S(2)}, u32[]{:S(2)}) %collective-permute-start.5) | collective-permute-done | bytes 172064 | tf_op jit(solution)/shard_map/ppermute | solution.py:241
  34.4 3.4 %collective-permute-done.6.rm = s32[56,768]{1,0:T(8,128)S(1)} collective-permute-done((s32[56,768]{1,0:T(8,128)S(1)}, s32[56,768]{1,0:T(8,128)S(1)}, u32[]{:S(2)}, u32[]{:S(2)}) %collective-permute-start.6) | collective-permute-done | bytes 172064 | tf_op jit(solution)/shard_map/ppermute | solution.py:241
  37.8 0.0 collective-permute-done.7.r2
  37.8 11.0 %shard_map.39 = f32[32,256]{1,0:T(8,128)S(1)} custom-call(s32[256,1]{1,0:T(8,128)S(1)} %reshape.10.idp, s32[96,768]{1,0:T(8,128)S(1)} %constant_dynamic-update-slice_fusion.pair, s32[16,768]{1,0:T(8,128)S(1)} %pad_add_fusion.hubs, s32[56,768]{1,0:T(8,128)S(1)} %constant_dynamic-update-slice_fusion.2.r0, s32[56,768]{1,0:T(8,128)S(1)} %collective-permute-done.5.rp, ...), custom_call_target="tpu_custom_call" | custom-call | flops 8589934592 | bytes 1048576 | tf_op jit(solution)/shard_map/pallas_call | solution.py:226
  48.9 14.3 %all_to_all.9 = f32[32,1,256]{2,1,0:T(1,128)S(1)} all-to-all(f32[32,1,256]{2,1,0:T(1,128)S(1)} %copy.8), channel_id=1, replica_groups=mesh['y'=4,'core'=2,'zh'=4,'x'=4,'zl'=2] {'zh','x','zl'}, dimensions={0} | all-to-all | bytes 65536 | tf_op jit(solution)/shard_map/all_to_all | solution.py:278
  63.2 0.1 reduce_sum.9
  63.3 0.5 add_divide_fusion
  (6 shorter events, 0.1 us)
Async XLA Ops:
  0.0 12.2 %collective-permute-start = (s32[48,768]{1,0:T(8,128)}, s32[48,768]{1,0:T(8,128)S(1)}, u32[]{:S(2)}, u32[]{:S(2)}) collective-permute-start(s32[48,768]{1,0:T(8,128)} %param.3), channel_id=1, source_target_pairs={{25,0},{8,1},{27,2},{10,3},{29,4},{12,5},{31,6},{14,7},{1,8},{16,9... | collective-permute-start | bytes 442376 | tf_op jit(solution)/shard_map/ppermute | solution.py:241
  5.9 17.7 %collective-permute-start.3 = (s32[48,768]{1,0:T(8,128)}, s32[48,768]{1,0:T(8,128)S(1)}, u32[]{:S(2)}, u32[]{:S(2)}) collective-permute-start(s32[48,768]{1,0:T(8,128)} %param.3), channel_id=1, source_target_pairs={{0,0},{25,1},{2,2},{27,3},{4,4},{29,5},{6,6},{31,7},{16,8},{9,9},{... | collective-permute-start | bytes 442376 | tf_op jit(solution)/shard_map/ppermute | solution.py:241
  7.8 8.1 %collective-permute-start.1 = (s32[4,768]{1,0:T(4,128)}, s32[4,768]{1,0:T(4,128)S(1)}, u32[]{:S(2)}, u32[]{:S(2)}) collective-permute-start(s32[4,768]{1,0:T(4,128)} %param.4), channel_id=1, source_target_pairs={{1,0},{0,1},{3,2},{2,3},{5,4},{4,5},{7,6},{6,7},{9,8},{8,9},{11,10... | collective-permute-start | bytes 36872 | tf_op jit(solution)/shard_map/ppermute | solution.py:241
  12.2 11.3 %collective-permute-start.8 = (s32[96,768]{1,0:T(8,128)S(1)}, s32[96,768]{1,0:T(8,128)S(1)}, u32[]{:S(2)}, u32[]{:S(2)}) collective-permute-start(s32[96,768]{1,0:T(8,128)S(1)} %constant_dynamic-update-slice_fusion.pair), channel_id=1, source_target_pairs={{0,0},{193,1},{2,2},{195,3},{4,4},{197,5},{6,6},{199,7},{136,8},{7... | collective-permute-start | bytes 884744 | tf_op jit(solution)/shard_map/ppermute | solution.py:241
  16.6 12.1 %collective-permute-start.2 = (s32[8,768]{1,0:T(8,128)S(1)}, s32[8,768]{1,0:T(8,128)S(1)}, u32[]{:S(2)}, u32[]{:S(2)}) collective-permute-start(s32[8,768]{1,0:T(8,128)S(1)} %pad_add_fusion.1), channel_id=1, source_target_pairs={{25,0},{8,1},{27,2},{10,3},{29,4},{12,5},{31,6},{14,7},{1,8},{16,9... | collective-permute-start | bytes 73736 | tf_op jit(solution)/shard_map/ppermute | solution.py:241
  16.8 6.9 %collective-permute-start.4 = (s32[8,768]{1,0:T(8,128)S(1)}, s32[8,768]{1,0:T(8,128)S(1)}, u32[]{:S(2)}, u32[]{:S(2)}) collective-permute-start(s32[8,768]{1,0:T(8,128)S(1)} %pad_add_fusion.1), channel_id=1, source_target_pairs={{0,0},{25,1},{2,2},{27,3},{4,4},{29,5},{6,6},{31,7},{16,8},{9,9},{... | collective-permute-start | bytes 73736 | tf_op jit(solution)/shard_map/ppermute | solution.py:241
  23.5 5.9 %collective-permute-start.9 = (s32[96,768]{1,0:T(8,128)S(1)}, s32[96,768]{1,0:T(8,128)S(1)}, u32[]{:S(2)}, u32[]{:S(2)}) collective-permute-start(s32[96,768]{1,0:T(8,128)S(1)} %collective-permute-done.8.words), channel_id=1, source_target_pairs={{32,0},{33,1},{34,2},{35,3},{36,4},{37,5},{38,6},{39,7},{40,8},{41... | collective-permute-start | bytes 884744 | tf_op jit(solution)/shard_map/ppermute | solution.py:241
  23.7 10.7 %collective-permute-start.5 = (s32[56,768]{1,0:T(8,128)S(1)}, s32[56,768]{1,0:T(8,128)S(1)}, u32[]{:S(2)}, u32[]{:S(2)}) collective-permute-start(s32[56,768]{1,0:T(8,128)S(1)} %constant_dynamic-update-slice_fusion.2.r0), channel_id=1, source_target_pairs={{2,0},{3,1},{4,2},{5,3},{6,4},{7,5},{0,6},{1,7},{10,8},{11,9},{12,... | collective-permute-start | bytes 516104 | tf_op jit(solution)/shard_map/ppermute | solution.py:241
  26.4 11.4 %collective-permute-start.6 = (s32[56,768]{1,0:T(8,128)S(1)}, s32[56,768]{1,0:T(8,128)S(1)}, u32[]{:S(2)}, u32[]{:S(2)}) collective-permute-start(s32[56,768]{1,0:T(8,128)S(1)} %constant_dynamic-update-slice_fusion.2.r0), channel_id=1, source_target_pairs={{6,0},{7,1},{0,2},{1,3},{2,4},{3,5},{4,6},{5,7},{14,8},{15,9},{8,1... | collective-permute-start | bytes 516104 | tf_op jit(solution)/shard_map/ppermute | solution.py:241
  26.5 11.4 %collective-permute-start.7 = (s32[56,768]{1,0:T(8,128)S(1)}, s32[56,768]{1,0:T(8,128)S(1)}, u32[]{:S(2)}, u32[]{:S(2)}) collective-permute-start(s32[56,768]{1,0:T(8,128)S(1)} %constant_dynamic-update-slice_fusion.2.r0), channel_id=1, source_target_pairs={{4,0},{5,1},{6,2},{7,3},{0,4},{1,5},{2,6},{3,7},{12,8},{13,9},{14,... | collective-permute-start | bytes 516104 | tf_op jit(solution)/shard_map/ppermute | solution.py:241
